TPU v7x, 32 devices: a whole 2x2x4 slice. The times are simulated.
32 devices in a mesh: seq: 16 (over z, y, core), slide: 2 (over x).
Axes of the slice: x: 2, y: 2, z: 4, core: 2. Of those that a mesh axis runs over, the one named last changes fastest.
Arguments:
- layer_input: bfloat16 [2, 4096, 768], P('slide', 'seq'), may hold values from -6 to 6
- cotangent: bfloat16 [2, 4096, 768], P('slide', 'seq'), may hold values from -6 to 6
- layer_norm_gain: float32 [768], replicated, may hold values from 0.25 to 1.75
- layer_norm_bias: float32 [768], replicated, may hold values from -3 to 3
- query_key_value_weight: bfloat16 [768, 2304], replicated, may hold values from -4 to 4
- output_weight: bfloat16 [768, 768], replicated, may hold values from -0.21875 to 0.21875
Outputs:
- layer_output: bfloat16 [2, 4096, 768], P('slide', 'seq')
- input_grad: bfloat16 [2, 4096, 768], P('slide', 'seq')
- grad_qkv: float32 [768, 2304], P('seq')
- grad_out: float32 [768, 768], P('seq')
- grad_gain: float32 [768], replicated
- grad_bias: float32 [768], replicated
All inputs are finite; a program needn't handle non-finite values.
Results may differ from a plain program's by a relative error of at most 0.011.
Values may be sent and summed in bfloat16 or wider, within the bound.
A program may use at most 128 MiB of HBM per device.

v0:
```python
import jax
import jax.numpy as jnp
from jax import lax
from jax.sharding import PartitionSpec as P

HEADS = 12


EPS = 1e-05


def from_behind(block, axis, distance):
    devices = range(lax.axis_size(axis))
    route = [(i - distance, i) for i in devices if i - distance in devices]
    return lax.ppermute(block, axis, route)


def apply_layer_norm(token_rows, scale_gain, shift_bias):
    values = token_rows.astype(jnp.float32)
    centered_rows = values - jnp.mean(values, axis=-1, keepdims=True)
    inverse_deviation = lax.rsqrt(
        jnp.mean(centered_rows * centered_rows, axis=-1, keepdims=True) + EPS
    )
    normalized_rows = centered_rows * inverse_deviation
    return (
        (normalized_rows * scale_gain + shift_bias).astype(jnp.bfloat16),
        normalized_rows,
        inverse_deviation,
    )


def attend(qkv_self, memory_key_value, memory_present):
    token_length = qkv_self.shape[0]
    feature_width = memory_key_value.shape[1] // 2
    head_dim = feature_width // HEADS
    query = qkv_self[:, :feature_width].reshape(token_length, HEADS, head_dim)
    keys = jnp.concatenate(
        [memory_key_value[:, :feature_width], qkv_self[:, feature_width : 2 * feature_width]], 0
    ).reshape(2 * token_length, HEADS, head_dim)
    values = jnp.concatenate(
        [memory_key_value[:, feature_width:], qkv_self[:, 2 * feature_width :]], 0
    ).reshape(2 * token_length, HEADS, head_dim)
    scores = jnp.einsum(
        "qhe,khe->hqk", query, keys, preferred_element_type=jnp.float32
    ) * head_dim ** (-0.5)
    row_ids = lax.broadcasted_iota(jnp.int32, (token_length, 2 * token_length), 0)
    col_ids = lax.broadcasted_iota(jnp.int32, (token_length, 2 * token_length), 1)
    allowed = jnp.where(col_ids < token_length, memory_present, col_ids - token_length <= row_ids)
    scores = jnp.where(allowed[None], scores, -1e30)
    top = jnp.max(scores, axis=-1, keepdims=True)
    weights = jnp.exp(scores - top)
    probs = weights / jnp.sum(weights, axis=-1, keepdims=True)
    probs_b = probs.astype(jnp.bfloat16)
    mixed = jnp.einsum("hqk,khe->qhe", probs_b, values, preferred_element_type=jnp.float32)
    mixed = mixed.reshape(token_length, feature_width).astype(jnp.bfloat16)
    return (mixed, probs, probs_b, query, keys, values)


def attend_back(d_mixed, probs, probs_b, query, keys, values):
    token_length, heads, head_dim = query.shape
    grad_heads = d_mixed.reshape(token_length, heads, head_dim)
    d_probs = jnp.einsum("qhe,khe->hqk", grad_heads, values, preferred_element_type=jnp.float32)
    d_scores = probs * (d_probs - jnp.sum(d_probs * probs, axis=-1, keepdims=True))
    d_scores_b = (d_scores * head_dim ** (-0.5)).astype(jnp.bfloat16)
    d_query = jnp.einsum("hqk,khe->qhe", d_scores_b, keys, preferred_element_type=jnp.float32)
    d_keys = jnp.einsum("hqk,qhe->khe", d_scores_b, query, preferred_element_type=jnp.float32)
    d_values = jnp.einsum("hqk,qhe->khe", probs_b, grad_heads, preferred_element_type=jnp.float32)
    return (
        d_query.reshape(token_length, -1).astype(jnp.bfloat16),
        d_keys.reshape(2 * token_length, -1).astype(jnp.bfloat16),
        d_values.reshape(2 * token_length, -1).astype(jnp.bfloat16),
    )


def block_forward(
    token_rows,
    gradient_list,
    current_query_key_value,
    memory_key_value,
    memory_present,
    current_normed,
    current_normalized,
    current_inverse_deviation,
    query_key_value_weight,
    output_weight,
    scale_gain,
):
    token_length = token_rows.shape[0]
    mixed, probs, probs_b, query, keys, values = attend(
        current_query_key_value, memory_key_value, memory_present
    )
    block_output = (
        token_rows.astype(jnp.float32)
        + jnp.dot(mixed, output_weight, preferred_element_type=jnp.float32)
    ).astype(jnp.bfloat16)
    d_mixed = jnp.dot(gradient_list, output_weight.T, preferred_element_type=jnp.float32).astype(
        jnp.bfloat16
    )
    grad_wout = jnp.dot(mixed.T, gradient_list, preferred_element_type=jnp.float32)
    d_query, d_keys, d_values = attend_back(d_mixed, probs, probs_b, query, keys, values)
    d_own = jnp.concatenate([d_query, d_keys[token_length:], d_values[token_length:]], 1)
    memory_gradient = jnp.concatenate([d_keys[:token_length], d_values[:token_length]], 1)
    grad_wqkv = jnp.dot(current_normed.T, d_own, preferred_element_type=jnp.float32)
    normed_gradient = jnp.dot(d_own, query_key_value_weight.T, preferred_element_type=jnp.float32)
    gain_gradient = jnp.sum(normed_gradient * current_normalized, axis=0)
    grad_b = jnp.sum(normed_gradient, axis=0)
    normalized_gradient = normed_gradient * scale_gain
    row_gradient = current_inverse_deviation * (
        normalized_gradient
        - jnp.mean(normalized_gradient, axis=-1, keepdims=True)
        - current_normalized
        * jnp.mean(normalized_gradient * current_normalized, axis=-1, keepdims=True)
    )
    input_gradient = (gradient_list.astype(jnp.float32) + row_gradient).astype(jnp.bfloat16)
    return (
        block_output,
        input_gradient,
        memory_gradient,
        (grad_wqkv, grad_wout, gain_gradient, grad_b),
    )


def memory_contributions(prior_normed, prior_normalized, memory_gradient, query_key_value_weight):
    feature_width = prior_normed.shape[1]
    key_value_gradient = jnp.dot(
        prior_normed.T, memory_gradient, preferred_element_type=jnp.float32
    )
    normed_gradient = jnp.dot(
        memory_gradient,
        query_key_value_weight[:, feature_width:].T,
        preferred_element_type=jnp.float32,
    )
    return (
        key_value_gradient,
        jnp.sum(normed_gradient * prior_normalized, axis=0),
        jnp.sum(normed_gradient, axis=0),
    )


def on_device(
    layer_input, cotangent, layer_norm_gain, layer_norm_bias, query_key_value_weight, output_weight
):
    token_rows = layer_input[0]
    gradient_list = cotangent[0]
    feature_width = token_rows.shape[1]
    normed_rows, normalized_rows, inverse_deviation = apply_layer_norm(
        token_rows, layer_norm_gain, layer_norm_bias
    )
    query_key_value = jnp.dot(
        normed_rows, query_key_value_weight, preferred_element_type=jnp.float32
    ).astype(jnp.bfloat16)
    has_first = lax.axis_index("seq") > 0
    previous_token_rows = from_behind(token_rows, "seq", 1)
    previous_normed_rows, previous_normalized, ignored_value = apply_layer_norm(
        previous_token_rows, layer_norm_gain, layer_norm_bias
    )
    kv_before = jnp.dot(
        previous_normed_rows,
        query_key_value_weight[:, feature_width:],
        preferred_element_type=jnp.float32,
    ).astype(jnp.bfloat16)
    block_output, input_gradient, memory_gradient, term_list = block_forward(
        token_rows,
        gradient_list,
        query_key_value,
        kv_before,
        has_first,
        normed_rows,
        normalized_rows,
        inverse_deviation,
        query_key_value_weight,
        output_weight,
        layer_norm_gain,
    )
    acc_qkv = term_list[0]
    acc_out = term_list[1]
    acc_gain = term_list[2]
    acc_bias = term_list[3]
    key_value_gradient, memory_gain, memory_bias = memory_contributions(
        previous_normed_rows, previous_normalized, memory_gradient, query_key_value_weight
    )
    acc_gain = acc_gain + memory_gain
    acc_bias = acc_bias + memory_bias
    combined = jnp.concatenate(
        [acc_qkv[:, :feature_width], acc_qkv[:, feature_width:] + key_value_gradient, acc_out], 1
    )
    seq_count = lax.axis_size("seq")
    slide_count = lax.axis_size("slide")
    factor = 1.0 / float(seq_count * slide_count * token_rows.shape[0]) ** 0.5
    gain_sum, bias_sum = lax.psum((acc_gain, acc_bias), ("seq", "slide"))
    shard = lax.psum_scatter(combined, "seq", scatter_dimension=0, tiled=True)
    shard = lax.psum(shard.astype(jnp.bfloat16), "slide").astype(jnp.float32)
    shard = shard * factor
    layer_output = block_output[None]
    input_grad = input_gradient[None]
    return (
        layer_output,
        input_grad,
        shard[:, : 3 * feature_width],
        shard[:, 3 * feature_width :],
        gain_sum * factor,
        bias_sum * factor,
    )


def solution(mesh):
    placed = (P("slide", "seq", None), P("slide", "seq", None), P(), P(), P(), P())
    return jax.shard_map(
        on_device,
        mesh=mesh,
        in_specs=placed,
        out_specs=(
            P("slide", "seq", None),
            P("slide", "seq", None),
            P("seq", None),
            P("seq", None),
            P(),
            P(),
        ),
        check_vma=False,
    )
```

profile of v0, /device:TPU:0, one launch (start us, length us, event | category | flops | bytes accessed | tf_op | source)
XLA Modules:
  0.0 261.9 jit_solution(17593352173310648972)
XLA Ops:
  7.2 0.0 reduce-scatter.2.cloned.1.call-start
  7.2 2.6 collective-permute-start
  9.8 1.1 convert_reduce_fusion
  10.9 1.2 fusion.65
  12.2 3.4 %convolution_convert_fusion = bf16[256,2304]{1,0:T(8,128)(2,1)S(1)} fusion(bf16[768,2304]{1,0:T(8,128)(2,1)} %param.10, f32[256]{0:T(256)S(1)} %add_rsqrt_fusion, f32[256]{0:T(256)S(1)} %broadcast_multiply_fusion.4, f32[768]{0:T(1024)} %param.9, f32[768]{0:T(1024)} %param.8, bf16[1,256,768]{2,1,0:T(8,128)(2,1)} %param.6), kind=kOutput, calls=%fused_computation.10 | convolution fusion | flops 907739136 | bytes 5120000 | tf_op jit(solution)/shard_map/dot_general | solution.py:149
  15.6 0.1 fusion.91
  15.7 1.3 convolution_convert_fusion.2
  17.0 0.5 iota_compare_fusion.1
  17.5 1.2 copy.24
  18.6 0.9 copy.22
  19.6 1.4 fusion.69
  21.0 0.1 convert_reduce_fusion.1
  21.1 0.2 fusion.66
  21.4 2.5 convolution_convert_fusion.1
  24.0 0.1 fusion.94
  24.0 1.3 pad_maximum_fusion.2
  25.3 1.4 copy.21
  26.7 2.3 copy.23
  29.0 6.7 %fusion.95 = (f32[12,256]{1,0:T(8,128)}, f32[12,256,512]{2,1,0:T(8,128)}) fusion(pred[256,512]{1,0:T(8,128)(4,1)} %fusion.69, bf16[256,12,64]{0,2,1:T(8,128)(2,1)S(1)} %bitcast.71, bf16[512,12,64]{0,2,1:T(8,128)(2,1)} %bitcast.69), kind=kOutput, calls=%fused_computation.104 | convolution fusion | flops 207618560 | bytes 7614464 | tf_op jit(solution)/shard_map/sub | solution.py:51
  35.7 4.1 %fusion.37 = bf16[12,64,256]{2,1,0:T(8,128)(2,1)S(1)} fusion(bf16[512,12,64]{0,2,1:T(8,128)(2,1)S(1)} %bitcast.55, f32[12,256,512]{2,1,0:T(8,128)} %get-tuple-element.24, f32[12,256]{1,0:T(8,128)} %get-tuple-element.23), kind=kOutput, calls=%fused_computation.33 | convolution fusion | flops 204668928 | bytes 7483392 | tf_op jit(solution)/shard_map/hqk,khe->qhe/dot_general | solution.py:54
  39.8 0.5 copy-done.20
  40.3 1.7 fusion.30
  42.1 3.7 %fusion.96 = f32[12,256,512]{2,1,0:T(8,128)} fusion(bf16[256,12,64]{0,2,1:T(8,128)(2,1)S(1)} %bitcast.58, bf16[512,12,64]{0,2,1:T(8,128)(2,1)S(1)} %bitcast.56), kind=kOutput, calls=%fused_computation.105 | convolution fusion | flops 201326592 | bytes 7471104 | tf_op jit(solution)/shard_map/qhe,khe->hqk/dot_general | solution.py:62
  45.7 22.5 %fusion.40 = bf16[12,64,256]{2,1,0:T(8,128)(2,1)} fusion(bf16[512,12,64]{0,2,1:T(8,128)(2,1)} %bitcast.70, f32[12,256,512]{2,1,0:T(8,128)} %fusion.96, f32[12,256,512]{2,1,0:T(8,128)} %get-tuple-element.24, f32[12,256]{1,0:T(8,128)} %get-tuple-element.23), kind=kOutput, calls=%fused_computation.34 | convolution fusion | flops 212536832 | bytes 13774848 | tf_op jit(solution)/shard_map/hqk,khe->qhe/dot_general | solution.py:65
  68.2 25.9 %fusion.33 = bf16[512,12,64]{0,2,1:T(8,128)(2,1)} fusion(bf16[256,12,64]{0,2,1:T(8,128)(2,1)S(1)} %bitcast.72, f32[12,256,512]{2,1,0:T(8,128)} %fusion.96, f32[12,256,512]{2,1,0:T(8,128)} %get-tuple-element.24, f32[12,256]{1,0:T(8,128)S(1)} %copy-done.22), kind=kOutput, calls=%fused_computation.30 | convolution fusion | flops 212733440 | bytes 13774848 | tf_op jit(solution)/shard_map/hqk,qhe->khe/dot_general | solution.py:66
  94.1 1.3 fusion.93
  95.4 1.9 fusion.73
  97.3 0.1 fusion.92
  97.4 1.3 fusion.70
  98.8 1.6 slice.80
  100.4 3.3 %slice_add_fusion = f32[768,1536]{1,0:T(8,128)} fusion(f32[768,2304]{1,0:T(8,128)S(1)} %fusion.70, bf16[256,768]{0,1:T(8,128)(2,1)S(1)} %bitcast.59, bf16[256,768]{0,1:T(8,128)(2,1)S(1)} %bitcast.61, bf16[256,768]{1,0:T(8,128)(2,1)S(1)} %collective-permute-done, f32[768]{0:T(1024)S(1)} %copy-done.13, f32[768]{0:T(1024)S(1)} %copy-done.12, ...), kind=kOutput, calls=%fused_computation.9 | convolution fusion | flops 607911936 | bytes 10625024 | tf_op jit(solution)/shard_map/dot_general | solution.py:125
  103.6 8.7 %pad_maximum_fusion = f32[768,3072]{1,0:T(8,128)} fusion(f32[768,768]{1,0:T(8,128)} %fusion.73, f32[768,1536]{1,0:T(8,128)} %slice_add_fusion, f32[768,768]{1,0:T(8,128)} %slice.80), kind=kLoop, calls=%fused_computation.2 | loop fusion | flops 4718592 | bytes 18874368 | tf_op jit(solution)/shard_map/concatenate | solution.py:184
  112.4 0.0 all-reduce.3.cloned.1.call-start
  112.4 0.6 copy-done.16
  113.1 2.7 %fusion.90 = (f32[768]{0:T(1024)S(1)}, f32[768]{0:T(1024)S(1)}) fusion(f32[256]{0:T(256)} %copy-done.17, f32[256]{0:T(256)S(1)} %copy-done.16, bf16[256,768]{1,0:T(8,128)(2,1)S(1)} %collective-permute-done, bf16[768,2304]{1,0:T(8,128)(2,1)} %param.10, bf16[256,768]{0,1:T(8,128)(2,1)S(1)} %bitcast.60, bf16[256,768]{0,1:T(8,128)(2,1)S(1)} %bitcast.62), kind=kOutput, calls=%fused_computation.99 | convolution fusion | flops 606730752 | bytes 3547136 | tf_op jit(solution)/shard_map/dot_general | solution.py:128
  115.8 0.4 copy-done.19
  116.1 1.4 fusion.64
  117.6 43.3 %all-reduce = (f32[768]{0:T(1024)S(1)}, f32[768]{0:T(1024)S(1)}) all-reduce(f32[768]{0:T(1024)S(1)} %add.62, f32[768]{0:T(1024)S(1)} %add.63), channel_id=1, replica_groups=mesh['seq'=16,'slide'=2] {'seq','slide'}, use_global_device_ids=true, to_apply=%region_13.14 | all-reduce | flops 1536 | bytes 12288 | tf_op jit(solution)/shard_map/psum | solution.py:190
  160.9 0.6 broadcast_multiply_fusion.1
  161.5 0.6 broadcast_multiply_fusion
  162.1 64.4 %reduce-scatter.2.cloned.1.call-done = f32[48,3072]{1,0:T(8,128)} async-done(((f32[768,3072]{1,0:T(8,128)}), f32[48,3072]{1,0:T(8,128)}) %reduce-scatter.2.cloned.1.call-update) | async-done | bytes 589840 | tf_op jit(solution)/shard_map/reduce_scatter | solution.py:191
  226.4 1.8 convert_element_type.99
  228.2 1.3 fusion.43
  229.5 1.1 fusion.72
  230.6 22.1 %all-reduce.3.cloned.1.call-done = bf16[48,3072]{1,0:T(8,128)(2,1)} async-done(((bf16[48,3072]{1,0:T(8,128)(2,1)}), bf16[48,3072]{1,0:T(8,128)(2,1)}) %all-reduce.3.cloned.1.call-update) | async-done | bytes 294928 | tf_op jit(solution)/shard_map/psum | solution.py:192
  252.6 1.0 convert_multiply_fusion
  253.6 0.7 slice.85
  254.3 0.8 slice.84
  (55 shorter events, 0.2 us)
Async XLA Ops:
  7.2 8.5 %copy-start = (bf16[768,768]{1,0:T(8,128)(2,1)S(1)}, bf16[768,768]{1,0:T(8,128)(2,1)}, u32[]{:S(2)}) copy-start(bf16[768,768]{1,0:T(8,128)(2,1)} %param.11) | copy-start | bytes 3538948
  7.2 219.2 %reduce-scatter.2.cloned.1.call-start = ((), (), s32[]{:S(2)}) async-start(), calls=%async_computation.1 | async-start | bytes 10027008 | tf_op jit(solution)/shard_map/reduce_scatter | solution.py:191
  7.2 13.7 %collective-permute-start = (bf16[256,768]{1,0:T(8,128)(2,1)}, bf16[256,768]{1,0:T(8,128)(2,1)S(1)}, u32[]{:S(2)}, u32[]{:S(2)}) collective-permute-start(bf16[256,768]{1,0:T(8,128)(2,1)} %bitcast.54), channel_id=1, source_target_pairs={{0,2},{2,4},{4,6},{6,8},{8,10},{10,12},{12,14},{14,16},{16,18},{18... | collective-permute-start | bytes 1179656 | tf_op jit(solution)/shard_map/ppermute | solution.py:15
  12.2 3.5 %copy-start.2 = (bf16[1,256,768]{2,1,0:T(8,128)(2,1)S(1)}, bf16[1,256,768]{2,1,0:T(8,128)(2,1)}, u32[]{:S(2)}) copy-start(bf16[1,256,768]{2,1,0:T(8,128)(2,1)} %param.7) | copy-start | bytes 1179652
  15.6 5.8 %copy-start.12 = (f32[768]{0:T(1024)S(1)}, f32[768]{0:T(1024)}, u32[]{:S(2)}) copy-start(f32[768]{0:T(1024)} %param.8) | copy-start | bytes 9220
  15.6 5.8 %copy-start.13 = (f32[768]{0:T(1024)S(1)}, f32[768]{0:T(1024)}, u32[]{:S(2)}) copy-start(f32[768]{0:T(1024)} %param.9) | copy-start | bytes 9220
  21.1 2.8 %copy-start.14 = (f32[256]{0:T(256)}, f32[256]{0:T(256)S(1)}, u32[]{:S(2)}) copy-start(f32[256]{0:T(256)S(1)} %broadcast_multiply_fusion.5) | copy-start | bytes 3076
  21.4 2.6 copy-start.17
  24.0 5.0 %copy-start.8 = (bf16[256,768]{0,1:T(8,128)(2,1)S(1)}, bf16[256,768]{0,1:T(8,128)(2,1)}, u32[]{:S(2)}) copy-start(bf16[256,768]{0,1:T(8,128)(2,1)} %copy.22) | copy-start | bytes 1179652
  35.7 4.6 %copy-start.20 = (f32[12,256,512]{2,1,0:T(8,128)S(1)}, f32[12,256,512]{2,1,0:T(8,128)}, u32[]{:S(2)}) copy-start(f32[12,256,512]{2,1,0:T(8,128)} %get-tuple-element.24) | copy-start | bytes 18874372
  35.7 4.6 %copy-start.21 = (f32[12,256]{1,0:T(8,128)S(1)}, f32[12,256]{1,0:T(8,128)}, u32[]{:S(2)}) copy-start(f32[12,256]{1,0:T(8,128)} %get-tuple-element.23) | copy-start | bytes 36868
  45.7 22.5 %copy-start.9 = (bf16[256,768]{0,1:T(8,128)(2,1)S(1)}, bf16[256,768]{0,1:T(8,128)(2,1)}, u32[]{:S(2)}) copy-start(bf16[256,768]{0,1:T(8,128)(2,1)} %copy.22) | copy-start | bytes 1179652
  45.7 22.5 %copy-start.22 = (f32[12,256]{1,0:T(8,128)S(1)}, f32[12,256]{1,0:T(8,128)}, u32[]{:S(2)}) copy-start(f32[12,256]{1,0:T(8,128)} %get-tuple-element.23) | copy-start | bytes 36868
  94.1 3.2 %copy-start.7 = (bf16[512,12,64]{0,2,1:T(8,128)(2,1)S(1)}, bf16[512,12,64]{0,2,1:T(8,128)(2,1)}, u32[]{:S(2)}) copy-start(bf16[512,12,64]{0,2,1:T(8,128)(2,1)} %fusion.33) | copy-start | bytes 2359300
  94.1 3.3 %copy-start.1 = (bf16[1,256,768]{2,1,0:T(8,128)(2,1)S(1)}, bf16[1,256,768]{2,1,0:T(8,128)(2,1)}, u32[]{:S(2)}) copy-start(bf16[1,256,768]{2,1,0:T(8,128)(2,1)} %param.6) | copy-start | bytes 1179652
  94.1 3.3 %copy-start.10 = (bf16[12,64,256]{2,1,0:T(8,128)(2,1)S(1)}, bf16[12,64,256]{2,1,0:T(8,128)(2,1)}, u32[]{:S(2)}) copy-start(bf16[12,64,256]{2,1,0:T(8,128)(2,1)} %fusion.40) | copy-start | bytes 1179652
  95.4 3.3 %copy-start.3 = (bf16[256,12,64]{0,2,1:T(8,128)(2,1)}, bf16[256,12,64]{0,2,1:T(8,128)(2,1)S(1)}, u32[]{:S(2)}) copy-start(bf16[256,12,64]{0,2,1:T(8,128)(2,1)S(1)} %get-tuple-element.20) | copy-start | bytes 1179652
  97.4 1.4 copy-start.5
  98.8 1.6 copy-start.15
  98.8 1.6 copy-start.18
  112.4 0.7 copy-start.16
  112.4 140.2 %all-reduce.3.cloned.1.call-start = ((), (), s32[]{:S(2)}) async-start(), calls=%async_computation.2 | async-start | bytes 589824 | tf_op jit(solution)/shard_map/psum | solution.py:192
  113.0 2.7 %copy-start.4 = (bf16[256,12,64]{0,2,1:T(8,128)(2,1)S(1)}, bf16[256,12,64]{0,2,1:T(8,128)(2,1)}, u32[]{:S(2)}) copy-start(bf16[256,12,64]{0,2,1:T(8,128)(2,1)} %copy-done.3) | copy-start | bytes 1179652
  113.1 2.7 %copy-start.6 = (bf16[256,12,64]{0,2,1:T(8,128)(2,1)S(1)}, bf16[256,12,64]{0,2,1:T(8,128)(2,1)}, u32[]{:S(2)}) copy-start(bf16[256,12,64]{0,2,1:T(8,128)(2,1)} %copy-done.5) | copy-start | bytes 1179652
  113.1 2.7 %copy-start.11 = (bf16[12,64,256]{2,1,0:T(8,128)(2,1)S(1)}, bf16[12,64,256]{2,1,0:T(8,128)(2,1)}, u32[]{:S(2)}) copy-start(bf16[12,64,256]{2,1,0:T(8,128)(2,1)} %fusion.40) | copy-start | bytes 1179652
  113.1 3.1 %copy-start.19 = (bf16[768,2304]{1,0:T(8,128)(2,1)S(1)}, bf16[768,2304]{1,0:T(8,128)(2,1)}, u32[]{:S(2)}) copy-start(bf16[768,2304]{1,0:T(8,128)(2,1)} %param.10) | copy-start | bytes 10616836
Sparse Core Ops, SparseCore 0:
  112.5 113.8 reduce-scatter.1
  229.3 23.3 all-reduce.2
where the time goes:
time: 263 us; the launch traced here: 262 us
  waiting for transfers between devices  86.4 us (33%)
  matrix products  83.5 us (32%)
  blocking collectives  43.3 us (16%)
  other arithmetic  19.8 us (8%)
  between operations  14.4 us (5%)
  local copies, waits for them, and re-layouts  11.9 us (5%)
  starting transfers between devices  2.63 us (1%)
    reduce_scatter x1, waiting for transfers between devices, on_device(): shard = lax.psum_scatter(combined, 'seq', scatter_dimension=0, tiled=True)  64.4 us
    psum x1, blocking collectives, on_device(): gain_sum, bias_sum = lax.psum((acc_gain, acc_bias), ('seq', 'slide'))  43.3 us
    dot_general x1, matrix products, attend_back(): jnp.einsum('hqk,qhe->khe', d_scores_b, query, preferred_element_type=jnp....  25.9 us
    dot_general x1, matrix products, attend_back(): jnp.einsum('hqk,khe->qhe', d_scores_b, keys, preferred_element_type=jnp.f...  22.5 us
    psum x1, waiting for transfers between devices, on_device(): shard = lax.psum(shard.astype(jnp.bfloat16), 'slide').astype(jnp.float32)  22.1 us
    concatenate x1, other arithmetic, on_device(): jnp.concatenate([acc_qkv[:, :feature_width], acc_qkv[:, feature_width:] +...  8.74 us
    sub x1, matrix products, attend(): weights = jnp.exp(scores - top)  6.67 us
  transfers between devices with their start and end apart: 3, of which 2 were waited for; matrix products, arithmetic and copies ran while one was open for 7% of the time, Pallas kernels for 0%

commit v1 on v0

v1 whole, which is shorter than its diff:
```python
import functools

import jax
import jax.numpy as jnp
from jax import lax
from jax.experimental import pallas as pl
from jax.experimental.pallas import tpu as pltpu
from jax.sharding import PartitionSpec as P

HEADS = 12
EPS = 1e-05
F32 = jnp.float32
BF16 = jnp.bfloat16
NT = (((1,), (1,)), ((), ()))
VMEM_LIMIT = 60 * 1024 * 1024


def dot(a, b):
    return jnp.dot(a, b, preferred_element_type=F32)


def dot_nt(a, b):
    return lax.dot_general(a, b, NT, preferred_element_type=F32)


def norm_rows(rows, gain, shift):
    values = rows.astype(F32)
    centered = values - jnp.mean(values, axis=-1, keepdims=True)
    rstd = lax.rsqrt(jnp.mean(centered * centered, axis=-1, keepdims=True) + EPS)
    xhat = centered * rstd
    return xhat * gain + shift, xhat, rstd


def layer_kernel(
    present_ref, x_ref, xp_ref, g_ref, gain_ref, bias_ref, w_ref, wo_ref,
    out_ref, dx_ref, grads_ref, vec_ref,
    normed_t, q_s, k_s, v_s, dm_s, mixed_t, d_s,
):
    tokens, width = x_ref.shape
    head = width // HEADS
    pair = 2 * head
    groups, slides, _, span = grads_ref.shape
    gain = gain_ref[...]
    shift = bias_ref[...]

    normed_f, _, _ = norm_rows(x_ref[...], gain, shift)
    prior_f, _, _ = norm_rows(xp_ref[...], gain, shift)
    normed = normed_f.astype(BF16)
    prior = prior_f.astype(BF16)
    normed_t[:, :tokens] = normed_f.T.astype(BF16)
    normed_t[:, tokens:] = prior_f.T.astype(BF16)
    scale = head ** (-0.5)
    q_s[...] = (dot(normed, w_ref[:, :width]).astype(BF16).astype(F32) * scale).astype(BF16)
    k_s[tokens:, :] = dot(normed, w_ref[:, width : 2 * width]).astype(BF16)
    v_s[tokens:, :] = dot(normed, w_ref[:, 2 * width :]).astype(BF16)
    k_s[:tokens, :] = dot(prior, w_ref[:, width : 2 * width]).astype(BF16)
    v_s[:tokens, :] = dot(prior, w_ref[:, 2 * width :]).astype(BF16)
    dm_s[...] = dot_nt(g_ref[...], wo_ref[...]).astype(BF16)

    missing = jnp.where(present_ref[0] > 0, 0.0, -1e30).astype(F32)
    key_ids = lax.broadcasted_iota(jnp.int32, (tokens, tokens), 0)
    query_ids = lax.broadcasted_iota(jnp.int32, (tokens, tokens), 1)
    seen = key_ids <= query_ids
    lanes = lax.broadcasted_iota(jnp.int32, (tokens, pair), 1)

    for p in range(HEADS // 2):
        cols = slice(p * pair, (p + 1) * pair)
        k2 = k_s[:, cols]
        v2 = v_s[:, cols]
        k2_t = k2.astype(F32).T.astype(BF16)
        v2_t = v2.astype(F32).T.astype(BF16)
        q2 = q_s[:, cols]
        dm2 = dm_s[:, cols]
        dk = None
        dv = None
        dq_rows = []
        for h in range(2):
            mine = (lanes < head) if h == 0 else (lanes >= head)
            qh = jnp.where(mine, q2, jnp.zeros_like(q2))
            dmh = jnp.where(mine, dm2, jnp.zeros_like(dm2))
            rows = slice(h * head, (h + 1) * head)
            s = dot_nt(k2, qh)
            s_mem = s[:tokens] + missing
            s_own = jnp.where(seen, s[tokens:], -1e30)
            top = jnp.maximum(
                jnp.max(s_mem, axis=0, keepdims=True), jnp.max(s_own, axis=0, keepdims=True)
            )
            e = jnp.concatenate([jnp.exp(s_mem - top), jnp.exp(s_own - top)], 0)
            probs = e * (1.0 / jnp.sum(e, axis=0, keepdims=True))
            probs_b = probs.astype(BF16)
            mixed_t[p * pair + h * head : p * pair + (h + 1) * head, :] = dot(
                v2_t[rows], probs_b
            ).astype(BF16)
            dp = dot_nt(v2, dmh)
            ds = probs * (dp - jnp.sum(dp * probs, axis=0, keepdims=True))
            ds_b = ds.astype(BF16)
            dq_rows.append(dot(k2_t[rows], ds_b))
            dk_h = dot(ds_b, qh)
            dv_h = dot(probs_b, dmh)
            dk = dk_h if dk is None else dk + dk_h
            dv = dv_h if dv is None else dv + dv_h
        dq = jnp.concatenate(dq_rows, 0).T * scale
        kc = slice(width + p * pair, width + (p + 1) * pair)
        vc = slice(2 * width + p * pair, 2 * width + (p + 1) * pair)
        d_s[:tokens, cols] = dq.astype(BF16)
        d_s[:tokens, kc] = dk[tokens:].astype(BF16)
        d_s[tokens:, kc] = dk[:tokens].astype(BF16)
        d_s[:tokens, vc] = dv[tokens:].astype(BF16)
        d_s[tokens:, vc] = dv[:tokens].astype(BF16)

    for b in range(groups * slides):
        lo = b * span
        if lo + span <= width:
            term = dot(normed_t[:, :tokens], d_s[:tokens, lo : lo + span])
        elif lo + span <= 3 * width:
            term = dot(normed_t[...], d_s[:, lo : lo + span])
        else:
            term = dot(mixed_t[...], g_ref[:, lo - 3 * width : lo - 3 * width + span])
        grads_ref[b // slides, b % slides] = term.astype(BF16)

    mixed = mixed_t[...].astype(F32).T.astype(BF16)
    out_ref[...] = (x_ref[...].astype(F32) + dot(mixed, wo_ref[...])).astype(BF16)

    d_prior = dot_nt(d_s[tokens:, width:], w_ref[:, width:])
    _, xhat_p, _ = norm_rows(xp_ref[...], gain, shift)
    vec_ref[0:1, :] = jnp.sum(d_prior * xhat_p, axis=0, keepdims=True)
    vec_ref[1:2, :] = jnp.sum(d_prior, axis=0, keepdims=True)
    d_own = dot_nt(d_s[:tokens, :], w_ref[...])
    _, xhat, rstd = norm_rows(x_ref[...], gain, shift)
    vec_ref[0:1, :] += jnp.sum(d_own * xhat, axis=0, keepdims=True)
    vec_ref[1:2, :] += jnp.sum(d_own, axis=0, keepdims=True)
    d_hat = d_own * gain
    d_row = rstd * (
        d_hat
        - jnp.mean(d_hat, axis=-1, keepdims=True)
        - xhat * jnp.mean(d_hat * xhat, axis=-1, keepdims=True)
    )
    dx_ref[...] = (g_ref[...].astype(F32) + d_row).astype(BF16)


def radices(count):
    found = []
    while count > 1:
        if len(found) < 2 and count % 2 == 0:
            step = 2
        else:
            step = 4 if count % 4 == 0 else (2 if count % 2 == 0 else count)
        found.append(step)
        count //= step
    return found


def plan(seq_count, slides):
    digits = []
    stride = 1
    for r in radices(seq_count):
        digits.append((r, stride))
        stride *= r
    axes = list(range(len(digits) + 1))
    first, rest = axes[:1], axes[1:]
    return digits + [(slides, 0)], first, rest


def reduce_kernel(digits, orders, grads_ref, vec_ref, full_ref, total_ref, *scratch):
    stages = len(digits)
    groups = len(orders)
    recv = [list(scratch[j * stages : (j + 1) * stages]) for j in range(groups)]
    at = groups * stages
    held = [list(scratch[at + j * stages : at + (j + 1) * stages]) for j in range(groups)]
    at += groups * stages
    vec_in = scratch[at : at + stages]
    at += stages
    send_sem, recv_sem, vsend_sem, vrecv_sem, gsend_sem, grecv_sem, local_sem = scratch[at:]
    seq = lax.axis_index("seq")
    slide = lax.axis_index("slide")
    slides = digits[-1][0]

    def digit(a):
        r, stride = digits[a]
        return slide if stride == 0 else lax.rem(lax.div(seq, stride), r)

    def peer(a, k):
        r, stride = digits[a]
        here = digit(a)
        there = lax.rem(here + k, r)
        if stride == 0:
            return there, (seq, there)
        return there, (seq + (there - here) * stride, slide)

    barrier = pltpu.get_barrier_semaphore()
    count = 0
    for a in range(stages):
        for k in range(1, digits[a][0]):
            pl.semaphore_signal(
                barrier, inc=1, device_id=peer(a, k)[1], device_id_type=pl.DeviceIdType.MESH
            )
            count += 1
    pl.semaphore_wait(barrier, count)

    def index_of(j, stage, value):
        order = orders[j]
        a = order[stage]
        left = sorted(order[stage:], reverse=True)
        pos = left.index(a)
        return tuple([slice(None)] * pos) + (value,)

    offsets = [[0] for _ in range(groups)]
    base = 0
    first = []
    for a in range(stages):
        first.append(base)
        base += digits[a][0] - 1

    def source(j, stage):
        return grads_ref.at[j] if stage == 0 else held[j][stage - 1]

    def copies(j, stage):
        a = orders[j][stage]
        made = []
        for k in range(1, digits[a][0]):
            there, dev = peer(a, k)
            made.append(
                pltpu.make_async_remote_copy(
                    src_ref=source(j, stage).at[index_of(j, stage, there)],
                    dst_ref=recv[j][stage].at[k - 1],
                    send_sem=send_sem.at[j, first[a] + k - 1],
                    recv_sem=recv_sem.at[j, first[a] + k - 1],
                    device_id=dev,
                    device_id_type=pl.DeviceIdType.MESH,
                )
            )
        return made

    def vec_copies(a):
        made = []
        for k in range(1, digits[a][0]):
            _, dev = peer(a, k)
            made.append(
                pltpu.make_async_remote_copy(
                    src_ref=vec_in[a].at[digit(a)],
                    dst_ref=vec_in[a].at[digit(a)],
                    send_sem=vsend_sem.at[first[a] + k - 1],
                    recv_sem=vrecv_sem.at[first[a] + k - 1],
                    device_id=dev,
                    device_id_type=pl.DeviceIdType.MESH,
                )
            )
        return made

    def gather_copies(j):
        made = []
        for k in range(1, slides):
            _, dev = peer(stages - 1, k)
            made.append(
                pltpu.make_async_remote_copy(
                    src_ref=full_ref.at[j, slide],
                    dst_ref=full_ref.at[j, slide],
                    send_sem=gsend_sem.at[j, k - 1],
                    recv_sem=grecv_sem.at[j, k - 1],
                    device_id=dev,
                    device_id_type=pl.DeviceIdType.MESH,
                )
            )
        return made

    live = {}
    for j in range(groups):
        live[j, 0] = copies(j, 0)
        for c in live[j, 0]:
            c.start()
    vec_in[0][digit(0)] = vec_ref[...]
    vec_live = [vec_copies(0)]
    for c in vec_live[0]:
        c.start()

    for stage in range(stages):
        for j in range(groups):
            a = orders[j][stage]
            for c in live[j, stage]:
                c.wait_recv()
            total = source(j, stage)[index_of(j, stage, digit(a))].astype(F32)
            for k in range(1, digits[a][0]):
                total = total + recv[j][stage][k - 1].astype(F32)
            if stage + 1 < stages:
                held[j][stage][...] = total.astype(BF16)
                live[j, stage + 1] = copies(j, stage + 1)
                for c in live[j, stage + 1]:
                    c.start()
            else:
                full_ref[j, slide] = total.astype(BF16)
                live[j, stage + 1] = gather_copies(j)
                for c in live[j, stage + 1]:
                    c.start()
        for c in vec_live[stage]:
            c.wait_recv()
        vec_total = vec_in[stage][0]
        for i in range(1, digits[stage][0]):
            vec_total = vec_total + vec_in[stage][i]
        if stage + 1 < stages:
            vec_in[stage + 1][digit(stage + 1)] = vec_total
            vec_live.append(vec_copies(stage + 1))
            for c in vec_live[-1]:
                c.start()
        else:
            total_ref[...] = vec_total

    for j in range(groups):
        for c in live[j, stages]:
            c.wait_recv()
    for made in list(live.values()) + vec_live:
        for c in made:
            c.wait_send()


def reduce_everywhere(grads, vec, seq_count, slides):
    groups = grads.shape[0]
    digits, head, rest = plan(seq_count, slides)
    stages = len(digits)
    orders = []
    for j in range(groups):
        turn = j % len(rest)
        orders.append(head + rest[turn:] + rest[:turn])
    width, span = grads.shape[2], grads.shape[3]
    rows = width // seq_count
    dims = [digits[a][0] for a in range(stages - 2, -1, -1)]
    shaped = grads.reshape([groups, slides] + dims + [rows, span])
    recv_shapes, held_shapes = [], []
    for j in range(groups):
        for stage in range(stages):
            a = orders[j][stage]
            after = [digits[b][0] for b in sorted(orders[j][stage + 1 :], reverse=True)]
            recv_shapes.append(pltpu.VMEM(tuple([digits[a][0] - 1] + after + [rows, span]), BF16))
            held_shapes.append(pltpu.VMEM(tuple(after + [rows, span]), BF16))
    vec_shapes = [pltpu.VMEM((digits[a][0],) + vec.shape, F32) for a in range(stages)]
    links = sum(r - 1 for r, _ in digits)
    dma = pltpu.SemaphoreType.DMA
    return pl.pallas_call(
        functools.partial(reduce_kernel, digits, orders),
        out_shape=(
            jax.ShapeDtypeStruct((groups, slides, rows, span), BF16),
            jax.ShapeDtypeStruct(vec.shape, F32),
        ),
        in_specs=[pl.BlockSpec(memory_space=pltpu.VMEM)] * 2,
        out_specs=(pl.BlockSpec(memory_space=pltpu.VMEM),) * 2,
        scratch_shapes=recv_shapes + held_shapes + vec_shapes + [
            dma((groups, links)), dma((groups, links)), dma((links,)), dma((links,)),
            dma((groups, max(slides - 1, 1))), dma((groups, max(slides - 1, 1))), dma((1,)),
        ],
        compiler_params=pltpu.CompilerParams(
            collective_id=0, has_side_effects=True, vmem_limit_bytes=VMEM_LIMIT
        ),
        name="reduce_terms",
    )(shaped, vec)


def on_device(x, g, gain, shift, w, wo):
    seq_count = lax.axis_size("seq")
    slides = lax.axis_size("slide")
    x = x[0]
    g = g[0]
    tokens, width = x.shape
    route = [(i, i + 1) for i in range(seq_count - 1)]
    xp = lax.ppermute(x, "seq", route)
    present = (lax.axis_index("seq") > 0).astype(jnp.int32).reshape(1)
    groups = 4
    span = 4 * width // (groups * slides)
    vmem = pl.BlockSpec(memory_space=pltpu.VMEM)
    out, dx, grads, vec = pl.pallas_call(
        layer_kernel,
        out_shape=(
            jax.ShapeDtypeStruct((tokens, width), BF16),
            jax.ShapeDtypeStruct((tokens, width), BF16),
            jax.ShapeDtypeStruct((groups, slides, width, span), BF16),
            jax.ShapeDtypeStruct((2, width), F32),
        ),
        in_specs=[pl.BlockSpec(memory_space=pltpu.SMEM)] + [vmem] * 7,
        out_specs=(vmem,) * 4,
        scratch_shapes=[
            pltpu.VMEM((width, 2 * tokens), BF16),
            pltpu.VMEM((tokens, width), BF16),
            pltpu.VMEM((2 * tokens, width), BF16),
            pltpu.VMEM((2 * tokens, width), BF16),
            pltpu.VMEM((tokens, width), BF16),
            pltpu.VMEM((width, tokens), BF16),
            pltpu.VMEM((2 * tokens, 3 * width), BF16),
        ],
        compiler_params=pltpu.CompilerParams(vmem_limit_bytes=VMEM_LIMIT),
        name="layer",
    )(present, x, xp, g, gain.reshape(1, width), shift.reshape(1, width), w, wo)
    full, total = reduce_everywhere(grads, vec, seq_count, slides)
    factor = 1.0 / float(seq_count * slides * tokens) ** 0.5
    rows = width // seq_count
    shard = full.astype(F32) * factor
    shard = shard.transpose(2, 0, 1, 3).reshape(rows, 4 * width)
    return (
        out[None],
        dx[None],
        shard[:, : 3 * width],
        shard[:, 3 * width :],
        total[0] * factor,
        total[1] * factor,
    )


def solution(mesh):
    placed = (P("slide", "seq", None), P("slide", "seq", None), P(), P(), P(), P())
    return jax.shard_map(
        on_device,
        mesh=mesh,
        in_specs=placed,
        out_specs=(
            P("slide", "seq", None),
            P("slide", "seq", None),
            P("seq", None),
            P("seq", None),
            P(),
            P(),
        ),
        check_vma=False,
    )
```

time: 263 us -> 83.3 us (0.32)
  waiting for transfers between devices: 86.4 us -> 0.01 us
  matrix products: 83.5 us -> 0 us
  Pallas kernels: 0 us -> 72.6 us
  blocking collectives: 43.3 us -> 0 us
  other arithmetic: 19.8 us -> 1.63 us
  between operations: 14.4 us -> 0.69 us
  local copies, waits for them, and re-layouts: 11.9 us -> 5.52 us
    dot_general x14 -> x0, matrix products: 76.8 us -> none  [the longest x1 25.9 us: attend_back(): jnp.einsum('hqk,qhe->khe', d_scores_b, query, preferred_element_type=jnp....]
    pallas_call x0 -> x2, Pallas kernels: none -> 72.6 us  [the longest x1 48.5 us: reduce_everywhere(): pl.pallas_call(functools.partial(reduce_kernel, digits, orders), out_shap...]
    reduce_scatter x1 -> x0, waiting for transfers between devices: 64.4 us -> none  [on_device(): shard = lax.psum_scatter(combined, 'seq', scatter_dimension=0, tiled=True)]
    psum x1 -> x0, blocking collectives: 43.3 us -> none  [on_device(): gain_sum, bias_sum = lax.psum((acc_gain, acc_bias), ('seq', 'slide'))]
    psum x1 -> x0, waiting for transfers between devices: 22.1 us -> none  [on_device(): shard = lax.psum(shard.astype(jnp.bfloat16), 'slide').astype(jnp.float32)]
    concatenate x2 -> x0, other arithmetic: 10 us -> none  [the longest x1 8.74 us: on_device(): jnp.concatenate([acc_qkv[:, :feature_width], acc_qkv[:, feature_width:] +...]
    sub x1 -> x0, matrix products: 6.67 us -> none  [attend(): weights = jnp.exp(scores - top)]
    slice x8 -> x2, local copies, waits for them, and re-layouts: 5.43 us -> 1.46 us  [the longest x1 0.79 us: on_device(): shard[:, :3 * width]]
  transfers between devices with their start and end apart: 3 -> 1, of which waited for: 2 -> 0; matrix products, arithmetic and copies ran while one was open for 7% -> 3% of each run, Pallas kernels for 0% -> 0%
where the time goes in v1:
time: 83.3 us; the launch traced here: 82.8 us
  Pallas kernels  72.6 us (87%)
  local copies, waits for them, and re-layouts  5.52 us (7%)
  starting transfers between devices  2.42 us (3%)
  other arithmetic  1.63 us (2%)
    pallas_call x1, Pallas kernels, reduce_everywhere(): pl.pallas_call(functools.partial(reduce_kernel, digits, orders), out_shap...  48.5 us
    pallas_call x1, Pallas kernels, on_device(): pl.pallas_call(layer_kernel, out_shape=(jax.ShapeDtypeStruct((tokens, wid...  24.1 us
    ppermute x1, starting transfers between devices, on_device(): xp = lax.ppermute(x, 'seq', route)  2.42 us
  transfers between devices with their start and end apart: 1, of which 0 were waited for; matrix products, arithmetic and copies ran while one was open for 3% of the time, Pallas kernels for 0%

profile of v1, /device:TPU:0, one launch (start us, length us, event | category | flops | bytes accessed | tf_op | source)
XLA Modules:
  0.0 82.8 jit_solution(5913097006773418118)
XLA Ops:
  0.6 2.4 %collective-permute-start = (bf16[256,768]{1,0:T(8,128)(2,1)}, bf16[256,768]{1,0:T(8,128)(2,1)S(1)}, u32[]{:S(2)}, u32[]{:S(2)}) collective-permute-start(bf16[256,768]{1,0:T(8,128)(2,1)} %bitcast.9), channel_id=1, source_target_pairs={{0,2},{2,4},{4,6},{6,8},{8,10},{10,12},{12,14},{14,16},{16,18},{18... | collective-permute-start | bytes 1179656 | tf_op jit(solution)/shard_map/ppermute | solution.py:363
  3.1 1.3 %reshape.35.gain_ref = f32[1,768]{1,0:T(1,128)} reshape(f32[768]{0:T(1024)} %param.8) | data formatting | bytes 6144 | tf_op jit(solution)/shard_map/reshape | solution.py:389
  4.3 1.3 %reshape.36.bias_ref = f32[1,768]{1,0:T(1,128)} reshape(f32[768]{0:T(1024)} %param.9) | data formatting | bytes 6144 | tf_op jit(solution)/shard_map/reshape | solution.py:389
  5.6 0.0 collective-permute-done.xp_ref
  5.6 0.0 copy-start
  5.6 0.7 copy-done
  6.4 24.1 %layer.1 = (bf16[256,768]{1,0:T(8,128)(2,1)}, bf16[256,768]{1,0:T(8,128)(2,1)}, bf16[4,2,768,384]{3,2,1,0:T(8,128)(2,1)}, f32[2,768]{1,0:T(2,128)}) custom-call(s32[1]{0:T(128)} %bitcast.present_ref, bf16[256,768]{1,0:T(8,128)(2,1)} %bitcast.10, bf16[256,768]{1,0:T(8,128)(2,1)} %copy-done, bf16[256,768]{1,0:T(8,128)(2,1)} %bitcast.11, ...), custom_call_target="tpu_custom_call" | custom-call | tf_op jit(solution)/shard_map/layer/pallas_call | solution.py:368
  30.4 48.5 %reduce_terms.1 = (bf16[4,2,48,384]{3,2,1,0:T(8,128)(2,1)}, f32[2,768]{1,0:T(2,128)}) custom-call(bf16[4,2,4,2,2,48,384]{6,5,4,3,2,1,0:T(8,128)(2,1)} %bitcast.8, f32[2,768]{1,0:T(2,128)} %get-tuple-element.15.vec_ref), custom_call_target="tpu_custom_call" | custom-call | tf_op jit(solution)/shard_map/reduce_terms/pallas_call | solution.py:337
  78.9 0.0 copy-start.1
  78.9 1.0 %multiply_bitcast_fusion = f32[48,4,2,384]{3,0,2,1:T(8,128)S(1)} fusion(bf16[4,2,48,384]{3,2,1,0:T(8,128)(2,1)} %get-tuple-element.16), kind=kLoop, calls=%fused_computation | loop fusion | flops 294912 | bytes 884736 | tf_op jit(solution)/shard_map/transpose | solution.py:394
  80.0 0.3 copy.12
  80.3 0.5 reshape.38
  80.8 0.7 slice.17
  81.4 0.8 slice.16
  82.2 0.0 copy-done.1
  82.2 0.6 multiply_reduce_fusion
Async XLA Ops:
  0.6 5.0 %collective-permute-start = (bf16[256,768]{1,0:T(8,128)(2,1)}, bf16[256,768]{1,0:T(8,128)(2,1)S(1)}, u32[]{:S(2)}, u32[]{:S(2)}) collective-permute-start(bf16[256,768]{1,0:T(8,128)(2,1)} %bitcast.9), channel_id=1, source_target_pairs={{0,2},{2,4},{4,6},{6,8},{8,10},{10,12},{12,14},{14,16},{16,18},{18... | collective-permute-start | bytes 1179656 | tf_op jit(solution)/shard_map/ppermute | solution.py:363
  5.6 0.7 copy-start
  78.9 3.3 %copy-start.1 = (f32[2,768]{1,0:T(2,128)S(1)}, f32[2,768]{1,0:T(2,128)}, u32[]{:S(2)}) copy-start(f32[2,768]{1,0:T(2,128)} %get-tuple-element.17) | copy-start | bytes 18436

commit v2 on v1

--- a/solution.py
+++ b/solution.py
@@ -31,33 +31,56 @@
     return xhat * gain + shift, xhat, rstd
 
 
-def layer_kernel(
-    present_ref, x_ref, xp_ref, g_ref, gain_ref, bias_ref, w_ref, wo_ref,
+def run_layer(
+    x_ref, xp_ref, g_ref, gain_ref, bias_ref, w_ref, wo_ref,
     out_ref, dx_ref, grads_ref, vec_ref,
     normed_t, q_s, k_s, v_s, dm_s, mixed_t, d_s,
+    blocks, await_prior, launch, advance,
 ):
     tokens, width = x_ref.shape
     head = width // HEADS
     pair = 2 * head
-    groups, slides, _, span = grads_ref.shape
+    slides = grads_ref.shape[1]
+    span = grads_ref.shape[-1]
+    dims = grads_ref.shape[2:-2]
+    rows_each = grads_ref.shape[-2]
     gain = gain_ref[...]
     shift = bias_ref[...]
 
     normed_f, _, _ = norm_rows(x_ref[...], gain, shift)
-    prior_f, _, _ = norm_rows(xp_ref[...], gain, shift)
     normed = normed_f.astype(BF16)
-    prior = prior_f.astype(BF16)
     normed_t[:, :tokens] = normed_f.T.astype(BF16)
-    normed_t[:, tokens:] = prior_f.T.astype(BF16)
     scale = head ** (-0.5)
     q_s[...] = (dot(normed, w_ref[:, :width]).astype(BF16).astype(F32) * scale).astype(BF16)
     k_s[tokens:, :] = dot(normed, w_ref[:, width : 2 * width]).astype(BF16)
     v_s[tokens:, :] = dot(normed, w_ref[:, 2 * width :]).astype(BF16)
+    dm_s[...] = dot_nt(g_ref[...], wo_ref[...]).astype(BF16)
+    await_prior()
+    prior_f, _, _ = norm_rows(xp_ref[...], gain, shift)
+    prior = prior_f.astype(BF16)
+    normed_t[:, tokens:] = prior_f.T.astype(BF16)
     k_s[:tokens, :] = dot(prior, w_ref[:, width : 2 * width]).astype(BF16)
     v_s[:tokens, :] = dot(prior, w_ref[:, 2 * width :]).astype(BF16)
-    dm_s[...] = dot_nt(g_ref[...], wo_ref[...]).astype(BF16)
-
-    missing = jnp.where(present_ref[0] > 0, 0.0, -1e30).astype(F32)
+
+    def emit(j):
+        for half in range(slides):
+            lo = blocks[j * slides + half] * span
+            if lo + span <= width:
+                term = dot(normed_t[:, :tokens], d_s[:tokens, lo : lo + span])
+            elif lo + span <= 3 * width:
+                term = dot(normed_t[...], d_s[:, lo : lo + span])
+            else:
+                term = dot(mixed_t[...], g_ref[:, lo - 3 * width : lo - 3 * width + span])
+            for i in range(width // rows_each):
+                at, left = [], i
+                for r in reversed(dims):
+                    at.append(left % r)
+                    left //= r
+                piece = term[i * rows_each : (i + 1) * rows_each].astype(BF16)
+                grads_ref[(j, half) + tuple(reversed(at))] = piece
+        launch(j)
+
+    missing = jnp.where(lax.axis_index("seq") > 0, 0.0, -1e30).astype(F32)
     key_ids = lax.broadcasted_iota(jnp.int32, (tokens, tokens), 0)
     query_ids = lax.broadcasted_iota(jnp.int32, (tokens, tokens), 1)
     seen = key_ids <= query_ids
@@ -108,19 +131,16 @@
         d_s[:tokens, vc] = dv[tokens:].astype(BF16)
         d_s[tokens:, vc] = dv[:tokens].astype(BF16)
 
-    for b in range(groups * slides):
-        lo = b * span
-        if lo + span <= width:
-            term = dot(normed_t[:, :tokens], d_s[:tokens, lo : lo + span])
-        elif lo + span <= 3 * width:
-            term = dot(normed_t[...], d_s[:, lo : lo + span])
-        else:
-            term = dot(mixed_t[...], g_ref[:, lo - 3 * width : lo - 3 * width + span])
-        grads_ref[b // slides, b % slides] = term.astype(BF16)
-
+        if p == HEADS // 4 - 1:
+            emit(0)
+
+    for j in range(1, grads_ref.shape[0]):
+        emit(j)
+        advance(j - 1)
     mixed = mixed_t[...].astype(F32).T.astype(BF16)
     out_ref[...] = (x_ref[...].astype(F32) + dot(mixed, wo_ref[...])).astype(BF16)
 
+    advance(grads_ref.shape[0] - 1)
     d_prior = dot_nt(d_s[tokens:, width:], w_ref[:, width:])
     _, xhat_p, _ = norm_rows(xp_ref[...], gain, shift)
     vec_ref[0:1, :] = jnp.sum(d_prior * xhat_p, axis=0, keepdims=True)
@@ -161,7 +181,13 @@
     return digits + [(slides, 0)], first, rest
 
 
-def reduce_kernel(digits, orders, grads_ref, vec_ref, full_ref, total_ref, *scratch):
+def sublayer_kernel(
+    digits, orders, blocks, factor,
+    x_ref, g_ref, gain_ref, bias_ref, w_ref, wo_ref,
+    out_ref, dx_ref, qkv_ref, proj_ref, total_ref,
+    grads_ref, vec_ref, full_ref, xp_ref, px_send, px_recv, *scratch,
+):
+    work, scratch = scratch[:7], scratch[7:]
     stages = len(digits)
     groups = len(orders)
     recv = [list(scratch[j * stages : (j + 1) * stages]) for j in range(groups)]
@@ -170,7 +196,7 @@
     at += groups * stages
     vec_in = scratch[at : at + stages]
     at += stages
-    send_sem, recv_sem, vsend_sem, vrecv_sem, gsend_sem, grecv_sem, local_sem = scratch[at:]
+    send_sem, recv_sem, vsend_sem, vrecv_sem, gsend_sem, grecv_sem = scratch[at:]
     seq = lax.axis_index("seq")
     slide = lax.axis_index("slide")
     slides = digits[-1][0]
@@ -195,7 +221,19 @@
                 barrier, inc=1, device_id=peer(a, k)[1], device_id_type=pl.DeviceIdType.MESH
             )
             count += 1
-    pl.semaphore_wait(barrier, count)
+    seq_count = lax.axis_size("seq")
+    ahead = lax.rem(seq + 1, seq_count)
+    behind = lax.rem(seq + seq_count - 1, seq_count)
+    for other in (ahead, behind):
+        pl.semaphore_signal(
+            barrier, inc=1, device_id=(other, slide), device_id_type=pl.DeviceIdType.MESH
+        )
+    pl.semaphore_wait(barrier, count + 2)
+    prior_copy = pltpu.make_async_remote_copy(
+        src_ref=x_ref, dst_ref=xp_ref, send_sem=px_send.at[0], recv_sem=px_recv.at[0],
+        device_id=(ahead, slide), device_id_type=pl.DeviceIdType.MESH,
+    )
+    prior_copy.start()
 
     def index_of(j, stage, value):
         order = orders[j]
@@ -264,66 +302,97 @@
         return made
 
     live = {}
-    for j in range(groups):
+    vec_live = []
+
+    def launch(j):
         live[j, 0] = copies(j, 0)
         for c in live[j, 0]:
             c.start()
-    vec_in[0][digit(0)] = vec_ref[...]
-    vec_live = [vec_copies(0)]
-    for c in vec_live[0]:
-        c.start()
-
-    for stage in range(stages):
+
+    def step(stage, j):
+        a = orders[j][stage]
+        for c in live[j, stage]:
+            c.wait_recv()
+        total = source(j, stage)[index_of(j, stage, digit(a))].astype(F32)
+        for k in range(1, digits[a][0]):
+            total = total + recv[j][stage][k - 1].astype(F32)
+        if stage + 1 < stages:
+            held[j][stage][...] = total.astype(BF16)
+            live[j, stage + 1] = copies(j, stage + 1)
+        else:
+            full_ref[j, slide] = total.astype(BF16)
+            live[j, stage + 1] = gather_copies(j)
+        for c in live[j, stage + 1]:
+            c.start()
+
+    def advance(diagonal):
         for j in range(groups):
-            a = orders[j][stage]
-            for c in live[j, stage]:
-                c.wait_recv()
-            total = source(j, stage)[index_of(j, stage, digit(a))].astype(F32)
-            for k in range(1, digits[a][0]):
-                total = total + recv[j][stage][k - 1].astype(F32)
-            if stage + 1 < stages:
-                held[j][stage][...] = total.astype(BF16)
-                live[j, stage + 1] = copies(j, stage + 1)
-                for c in live[j, stage + 1]:
-                    c.start()
-            else:
-                full_ref[j, slide] = total.astype(BF16)
-                live[j, stage + 1] = gather_copies(j)
-                for c in live[j, stage + 1]:
-                    c.start()
+            if 0 <= diagonal - j < stages:
+                step(diagonal - j, j)
+
+    def vec_start(stage, value):
+        vec_in[stage][digit(stage)] = value
+        vec_live.append(vec_copies(stage))
+        for c in vec_live[-1]:
+            c.start()
+
+    def vec_step(stage):
         for c in vec_live[stage]:
             c.wait_recv()
-        vec_total = vec_in[stage][0]
+        value = vec_in[stage][0]
         for i in range(1, digits[stage][0]):
-            vec_total = vec_total + vec_in[stage][i]
+            value = value + vec_in[stage][i]
         if stage + 1 < stages:
-            vec_in[stage + 1][digit(stage + 1)] = vec_total
-            vec_live.append(vec_copies(stage + 1))
-            for c in vec_live[-1]:
-                c.start()
+            vec_start(stage + 1, value)
         else:
-            total_ref[...] = vec_total
-
+            total_ref[...] = value
+
+    run_layer(
+        x_ref, xp_ref, g_ref, gain_ref, bias_ref, w_ref, wo_ref, out_ref, dx_ref,
+        grads_ref, vec_ref, *work, blocks, prior_copy.wait_recv, launch, advance,
+    )
+    vec_start(0, vec_ref[...])
+    done = 0
+    for diagonal in range(groups, stages + groups - 1):
+        advance(diagonal)
+        if done < stages:
+            vec_step(done)
+            done += 1
+    for stage in range(done, stages):
+        vec_step(stage)
+    span = full_ref.shape[-1]
     for j in range(groups):
         for c in live[j, stages]:
             c.wait_recv()
+        for half in range(slides):
+            lo = blocks[j * slides + half] * span
+            value = full_ref[j, half].astype(F32) * factor
+            if lo < qkv_ref.shape[1]:
+                qkv_ref[:, lo : lo + span] = value
+            else:
+                lo -= qkv_ref.shape[1]
+                proj_ref[:, lo : lo + span] = value
+    prior_copy.wait_send()
     for made in list(live.values()) + vec_live:
         for c in made:
             c.wait_send()
 
 
-def reduce_everywhere(grads, vec, seq_count, slides):
-    groups = grads.shape[0]
+def on_device(x, g, gain, shift, w, wo):
+    seq_count = lax.axis_size("seq")
+    slides = lax.axis_size("slide")
+    tokens, width = x.shape[1:]
+    groups = 8 // slides
+    blocks = (0, 2, 4, 1, 3, 5, 6, 7)
+    span = width // 2
+    factor = 1.0 / float(seq_count * slides * tokens) ** 0.5
     digits, head, rest = plan(seq_count, slides)
     stages = len(digits)
-    orders = []
-    for j in range(groups):
-        turn = j % len(rest)
-        orders.append(head + rest[turn:] + rest[:turn])
-    width, span = grads.shape[2], grads.shape[3]
+    near, far, last = rest[0], rest[1:-1], rest[-1]
+    kinds = [[last, near] + far, [near, last] + far, [last] + far + [near], [near] + far + [last]]
+    orders = [head + kinds[j % len(kinds)] for j in range(groups)]
     rows = width // seq_count
     dims = [digits[a][0] for a in range(stages - 2, -1, -1)]
-    shaped = grads.reshape([groups, slides] + dims + [rows, span])
     recv_shapes, held_shapes = [], []
     for j in range(groups):
         for stage in range(stages):
@@ -331,51 +400,28 @@
             after = [digits[b][0] for b in sorted(orders[j][stage + 1 :], reverse=True)]
             recv_shapes.append(pltpu.VMEM(tuple([digits[a][0] - 1] + after + [rows, span]), BF16))
             held_shapes.append(pltpu.VMEM(tuple(after + [rows, span]), BF16))
-    vec_shapes = [pltpu.VMEM((digits[a][0],) + vec.shape, F32) for a in range(stages)]
+    vec_shapes = [pltpu.VMEM((digits[a][0], 2, width), F32) for a in range(stages)]
     links = sum(r - 1 for r, _ in digits)
     dma = pltpu.SemaphoreType.DMA
-    return pl.pallas_call(
-        functools.partial(reduce_kernel, digits, orders),
-        out_shape=(
-            jax.ShapeDtypeStruct((groups, slides, rows, span), BF16),
-            jax.ShapeDtypeStruct(vec.shape, F32),
-        ),
-        in_specs=[pl.BlockSpec(memory_space=pltpu.VMEM)] * 2,
-        out_specs=(pl.BlockSpec(memory_space=pltpu.VMEM),) * 2,
-        scratch_shapes=recv_shapes + held_shapes + vec_shapes + [
-            dma((groups, links)), dma((groups, links)), dma((links,)), dma((links,)),
-            dma((groups, max(slides - 1, 1))), dma((groups, max(slides - 1, 1))), dma((1,)),
-        ],
-        compiler_params=pltpu.CompilerParams(
-            collective_id=0, has_side_effects=True, vmem_limit_bytes=VMEM_LIMIT
-        ),
-        name="reduce_terms",
-    )(shaped, vec)
-
-
-def on_device(x, g, gain, shift, w, wo):
-    seq_count = lax.axis_size("seq")
-    slides = lax.axis_size("slide")
-    x = x[0]
-    g = g[0]
-    tokens, width = x.shape
-    route = [(i, i + 1) for i in range(seq_count - 1)]
-    xp = lax.ppermute(x, "seq", route)
-    present = (lax.axis_index("seq") > 0).astype(jnp.int32).reshape(1)
-    groups = 4
-    span = 4 * width // (groups * slides)
     vmem = pl.BlockSpec(memory_space=pltpu.VMEM)
-    out, dx, grads, vec = pl.pallas_call(
-        layer_kernel,
+    out, dx, qkv, proj, total = pl.pallas_call(
+        functools.partial(sublayer_kernel, digits, orders, blocks, factor),
         out_shape=(
             jax.ShapeDtypeStruct((tokens, width), BF16),
             jax.ShapeDtypeStruct((tokens, width), BF16),
-            jax.ShapeDtypeStruct((groups, slides, width, span), BF16),
+            jax.ShapeDtypeStruct((rows, 3 * width), F32),
+            jax.ShapeDtypeStruct((rows, width), F32),
             jax.ShapeDtypeStruct((2, width), F32),
         ),
-        in_specs=[pl.BlockSpec(memory_space=pltpu.SMEM)] + [vmem] * 7,
-        out_specs=(vmem,) * 4,
+        in_specs=[vmem] * 6,
+        out_specs=(vmem,) * 5,
         scratch_shapes=[
+            pltpu.VMEM(tuple([groups, slides] + dims + [rows, span]), BF16),
+            pltpu.VMEM((2, width), F32),
+            pltpu.VMEM((groups, slides, rows, span), BF16),
+            pltpu.VMEM((tokens, width), BF16),
+            dma((1,)),
+            dma((1,)),
             pltpu.VMEM((width, 2 * tokens), BF16),
             pltpu.VMEM((tokens, width), BF16),
             pltpu.VMEM((2 * tokens, width), BF16),
@@ -383,23 +429,16 @@
             pltpu.VMEM((tokens, width), BF16),
             pltpu.VMEM((width, tokens), BF16),
             pltpu.VMEM((2 * tokens, 3 * width), BF16),
+        ] + recv_shapes + held_shapes + vec_shapes + [
+            dma((groups, links)), dma((groups, links)), dma((links,)), dma((links,)),
+            dma((groups, max(slides - 1, 1))), dma((groups, max(slides - 1, 1))),
         ],
-        compiler_params=pltpu.CompilerParams(vmem_limit_bytes=VMEM_LIMIT),
-        name="layer",
-    )(present, x, xp, g, gain.reshape(1, width), shift.reshape(1, width), w, wo)
-    full, total = reduce_everywhere(grads, vec, seq_count, slides)
-    factor = 1.0 / float(seq_count * slides * tokens) ** 0.5
-    rows = width // seq_count
-    shard = full.astype(F32) * factor
-    shard = shard.transpose(2, 0, 1, 3).reshape(rows, 4 * width)
-    return (
-        out[None],
-        dx[None],
-        shard[:, : 3 * width],
-        shard[:, 3 * width :],
-        total[0] * factor,
-        total[1] * factor,
-    )
+        compiler_params=pltpu.CompilerParams(
+            collective_id=0, has_side_effects=True, vmem_limit_bytes=VMEM_LIMIT
+        ),
+        name="sublayer",
+    )(x[0], g[0], gain.reshape(1, width), shift.reshape(1, width), w, wo)
+    return (out[None], dx[None], qkv, proj, total[0] * factor, total[1] * factor)
 
 
 def solution(mesh):

time: 83.3 us -> 82.8 us (level)
  local copies, waits for them, and re-layouts: 5.52 us -> 9.45 us
  starting transfers between devices: 2.42 us -> 0 us
  Pallas kernels: 72.6 us -> 71 us
    unnamed x4, local copies, waits for them, and re-layouts: 0.75 us -> 6.91 us
    ppermute x1 -> x0, starting transfers between devices: 2.42 us -> none  [on_device(): xp = lax.ppermute(x, 'seq', route)]
    pallas_call x2 -> x1, Pallas kernels: 72.6 us -> 71 us  [on_device(): pl.pallas_call(functools.partial(sublayer_kernel, digits, orders, blocks,...]
    slice x2 -> x0, local copies, waits for them, and re-layouts: 1.46 us -> none  [the longest x1 0.79 us: on_device(): shard[:, :3 * width]]
    transpose x1 -> x0, other arithmetic: 1.02 us -> none  [on_device(): shard = shard.transpose(2, 0, 1, 3).reshape(rows, 4 * width)]
  transfers between devices with their start and end apart: 1 -> 0, of which waited for: 0 -> 0; matrix products, arithmetic and copies ran while one was open for 3% -> 0% of each run, Pallas kernels for 0% -> 0%
where the time goes in v2:
time: 82.8 us; the launch traced here: 82.4 us
  Pallas kernels  71 us (86%)
  local copies, waits for them, and re-layouts  9.45 us (11%)
  other arithmetic  1.39 us (2%)
    pallas_call x1, Pallas kernels, on_device(): pl.pallas_call(functools.partial(sublayer_kernel, digits, orders, blocks,...  71 us
    unnamed x4, local copies, waits for them, and re-layouts  6.91 us

profile of v2, /device:TPU:0, one launch (start us, length us, event | category | flops | bytes accessed | tf_op | source)
XLA Modules:
  0.0 82.4 jit_solution(13899291986493669189)
XLA Ops:
  0.6 1.3 %reshape.22.gain_ref = f32[1,768]{1,0:T(1,128)} reshape(f32[768]{0:T(1024)} %param.8) | data formatting | bytes 6144 | tf_op jit(solution)/shard_map/reshape | solution.py:440
  1.9 1.3 %reshape.23.bias_ref = f32[1,768]{1,0:T(1,128)} reshape(f32[768]{0:T(1024)} %param.9) | data formatting | bytes 6144 | tf_op jit(solution)/shard_map/reshape | solution.py:440
  3.2 71.0 %sublayer.1 = (bf16[256,768]{1,0:T(8,128)(2,1)}, bf16[256,768]{1,0:T(8,128)(2,1)}, f32[48,2304]{1,0:T(8,128)}, f32[48,768]{1,0:T(8,128)}, f32[2,768]{1,0:T(2,128)}) custom-call(bf16[256,768]{1,0:T(8,128)(2,1)} %bitcast.4, bf16[256,768]{1,0:T(8,128)(2,1)} %bitcast.5, f32[1,768]{1,0:T(1,128)} %reshape.22.gain_ref, f32[1,768]{1,0:T(1,128)} %reshape.23.bias_ref, ...), custom_call_target="tpu_custom_call" | custom-call | tf_op jit(solution)/shard_map/sublayer/pallas_call | solution.py:407
  74.1 1.4 %multiply_reduce_fusion = (f32[768]{0:T(1024)}, f32[768]{0:T(1024)}) fusion(f32[2,768]{1,0:T(2,128)} %get-tuple-element.15), kind=kLoop, calls=%fused_computation | loop fusion | flops 1536 | bytes 12288 | tf_op jit(solution)/shard_map/mul | solution.py:441
  75.5 1.8 %copy.16 = bf16[1,256,768]{2,1,0:T(8,128)(2,1)} copy(bf16[1,256,768]{2,1,0:T(8,128)(2,1)} %bitcast.7) | data formatting | bytes 786432
  77.3 1.8 %copy.17 = bf16[1,256,768]{2,1,0:T(8,128)(2,1)} copy(bf16[1,256,768]{2,1,0:T(8,128)(2,1)} %bitcast.6) | data formatting | bytes 786432
  79.1 1.8 %copy.18 = f32[48,2304]{1,0:T(8,128)} copy(f32[48,2304]{1,0:T(8,128)} %get-tuple-element.26) | data formatting | bytes 884736
  80.9 1.6 %copy.19 = f32[48,768]{1,0:T(8,128)} copy(f32[48,768]{1,0:T(8,128)} %get-tuple-element.27) | data formatting | bytes 294912
